TPU v7x, 256 devices: a whole 4x4x8 slice. The times are simulated.
256 devices in a mesh: rows: 128 (over z, x, y), tgt: 2 (over core).
Axes of the slice: x: 4, y: 4, z: 8, core: 2. Of those that a mesh axis runs over, the one named last changes fastest.
Arguments:
- counts: int32 [128], P('rows'), may hold values from 512 to 2048, as said below
- samples: float32 [262144, 256], P('rows'), may hold values from -6 to 6
- targets: float32 [262144, 256], P('rows', 'tgt'), may hold values from -6 to 6
- point_ids: int32 [2, 512], replicated, may hold values from 0 to 262143, as said below
- block_inverse: float32 [2, 512, 512], replicated, may hold values from -4.7683716e-07 to 5.8716338e-06
Outputs:
- residual: float32 [262144, 256], P('rows', 'tgt')
Inputs may be any that keep to these rules, and one draw needn't show every extreme that they name: `counts`: some device has exactly 2048 live rows. `point_ids`: every id is d * 2048 + s with s < counts[d].
All inputs are finite; a program needn't handle non-finite values.
Results may differ from a plain program's by a relative error of at most 0.0003.
Values sent between devices are 32-bit elements; how exact they have to be, the bound alone decides.
A program may use at most 64 MiB of HBM per device.

v0:
```python
import jax
import jax.numpy as jnp
from jax import lax
from jax.sharding import Mesh
from jax.sharding import PartitionSpec as P

ROWS = ("rows_0", "rows_1", "rows_2")


def rows_for(lines, count):
    spare = -len(lines) % count
    return jnp.pad(lines, [(0, spare)] + [(0, 0)] * (lines.ndim - 1))


def sent_to_all(shard, axis):
    count = lax.axis_size(axis)
    return lax.all_to_all(
        jnp.broadcast_to(shard[None], (count, *shard.shape)), axis, 0, 0, tiled=True
    )


def joined_along(pieces, dim):
    pieces = jnp.moveaxis(pieces, 0, dim)
    shape = pieces.shape
    return pieces.reshape(*shape[:dim], shape[dim] * shape[dim + 1], *shape[dim + 2 :])


def gathered_by_axis(shard, axes, dim):
    far, near = axes
    first = sent_to_all(shard, far)
    pieces = jnp.swapaxes(sent_to_all(first, near), 0, 1)
    return joined_along(pieces.reshape(-1, *shard.shape), dim)


def in_blocks(shard, dim, count):
    before, after = (shard.shape[:dim], shard.shape[dim + 1 :])
    return jnp.moveaxis(shard.reshape(*before, count, -1, *after), dim, 0)


def summed_on_arrival(shard, axis, dim):
    pieces = in_blocks(shard, dim, lax.axis_size(axis))
    arrived = lax.all_to_all(pieces, axis, split_axis=0, concat_axis=0, tiled=True)
    return arrived.sum(axis=0)


def sum_in_two_steps(shard, axes, dim):
    far, near = axes
    pieces = in_blocks(shard, dim, lax.axis_size(far))
    nearer = summed_on_arrival(pieces, near, dim + 1)
    arrived = lax.all_to_all(nearer, far, split_axis=0, concat_axis=0, tiled=True)
    return arrived.sum(axis=0)


def sum_by_parts(shard, axes):
    lines = shard.reshape(-1, shard.shape[-1])
    padded = rows_for(lines, lax.axis_size(axes[0]) * lax.axis_size(axes[1]))
    whole = gathered_by_axis(sum_in_two_steps(padded, axes, 0), axes, 0)
    return lax.slice_in_dim(whole, 0, len(lines)).reshape(shard.shape)


def kernel_columns(rows_in, points):
    scaled = lax.dot_general(
        rows_in,
        points,
        (((1,), (1,)), ((), ())),
        precision=lax.Precision.HIGHEST,
        preferred_element_type=jnp.float32,
    )
    scaled = scaled * (1.0 / rows_in.shape[1] ** 0.5)
    return (0.5 * scaled + 1.0) ** 3


def pick_rows(samples, wanted, device):
    rows_here = samples.shape[0]
    local = wanted - device * rows_here
    owned = (local >= 0) & (local < rows_here)
    taken = jnp.take(samples, jnp.clip(local, 0, rows_here - 1), axis=0)
    return jnp.where(owned[:, None], taken, 0.0)


def on_device(counts, samples, targets, point_ids, block_inverse):
    rows_here = samples.shape[0]
    live_count = counts[0]
    device = lax.axis_index(ROWS)
    row_block = min(512, rows_here)
    loop_end = (live_count + row_block - 1) // row_block
    residual = targets
    block_size = point_ids.shape[1]
    for block_index in range(point_ids.shape[0]):
        wanted = point_ids[block_index]
        points = sum_by_parts(pick_rows(samples, wanted, device), (("rows_0", "rows_1"), "rows_2"))

        def accumulate(index, carry):
            stored, totals = carry
            start = index * row_block
            rows_in = lax.dynamic_slice_in_dim(samples, start, row_block, 0)
            current = lax.dynamic_slice_in_dim(residual, start, row_block, 0)
            slot_ids = start + jnp.arange(row_block, dtype=jnp.int32)
            columns = jnp.where(
                (slot_ids < live_count)[:, None], kernel_columns(rows_in, points), 0.0
            )
            totals = totals + lax.dot_general(
                columns,
                current,
                (((0,), (0,)), ((), ())),
                precision=lax.Precision.HIGHEST,
                preferred_element_type=jnp.float32,
            )
            stored = lax.dynamic_update_slice_in_dim(stored, columns, start, 0)
            return (stored, totals)

        start_state = (
            jnp.zeros((rows_here, block_size), jnp.float32),
            jnp.zeros((block_size, residual.shape[1]), jnp.float32),
        )
        stored, totals = lax.fori_loop(0, loop_end, accumulate, start_state)
        sums = sum_by_parts(totals, (("rows_0", "rows_1"), "rows_2"))
        coefs = jnp.dot(
            block_inverse[block_index],
            sums,
            precision=lax.Precision.HIGHEST,
            preferred_element_type=jnp.float32,
        )
        residual = residual - jnp.dot(
            stored, coefs, precision=lax.Precision.HIGHEST, preferred_element_type=jnp.float32
        )
    return residual


def solution(mesh):
    finer = Mesh(
        mesh.devices.reshape(8, 4, 4, mesh.shape["tgt"]), ("rows_0", "rows_1", "rows_2", "tgt")
    )
    placed = (P(ROWS), P(ROWS, None), P(ROWS, "tgt"), P(), P())
    return jax.shard_map(
        on_device, mesh=finer, in_specs=placed, out_specs=P(ROWS, "tgt"), check_vma=False
    )
```

profile of v0, /device:TPU:32, one launch (start us, length us, event | category | flops | bytes accessed | tf_op | source)
XLA Modules:
  0.0 282.1 jit_solution(250433483169284677)
XLA Ops:
  1.7 3.2 %gather_fusion = f32[512,256]{1,0:T(8,128)S(1)} fusion(f32[2048,256]{1,0:T(8,128)} %param.12, s32[1024]{0:T(1024)S(1)} %pad_clamp_fusion.1), kind=kCustom, calls=%fused_computation.clone | custom fusion | bytes 1050624 | tf_op jit(solution)/shard_map/jit(_take)/gather | solution.py:77
  9.9 4.5 %all-to-all-start = ((f32[4,32,4,256]{3,2,1,0:T(4,128)}), f32[4,32,4,256]{3,2,1,0:T(4,128)S(1)}, u32[]{:S(2)}, u32[]{:S(2)}) async-start(f32[4,32,4,256]{3,2,1,0:T(4,128)} %bitcast.50), calls=%async_computation | async-start | bytes 1048576 | tf_op jit(solution)/shard_map/all_to_all | solution.py:42
  14.3 9.5 %all-to-all-done = f32[4,32,4,256]{3,2,1,0:T(4,128)S(1)} async-done(((f32[4,32,4,256]{3,2,1,0:T(4,128)}), f32[4,32,4,256]{3,2,1,0:T(4,128)S(1)}, u32[]{:S(2)}, u32[]{:S(2)}) %all-to-all-start) | async-done | bytes 524320 | tf_op jit(solution)/shard_map/all_to_all | solution.py:42
  24.6 11.2 %all-to-all-start.1 = ((f32[32,4,256]{2,1,0:T(4,128)}), f32[32,4,256]{2,1,0:T(4,128)S(1)}, u32[]{:S(2)}, u32[]{:S(2)}) async-start(f32[32,4,256]{2,1,0:T(4,128)} %reduce_sum.72), calls=%async_computation.1 | async-start | bytes 262144 | tf_op jit(solution)/shard_map/all_to_all | solution.py:50
  36.8 8.6 %all-to-all-done.1 = f32[32,4,256]{2,1,0:T(4,128)S(1)} async-done(((f32[32,4,256]{2,1,0:T(4,128)}), f32[32,4,256]{2,1,0:T(4,128)S(1)}, u32[]{:S(2)}, u32[]{:S(2)}) %all-to-all-start.1) | async-done | bytes 131104 | tf_op jit(solution)/shard_map/all_to_all | solution.py:50
  45.3 3.5 %all-to-all-start.8 = ((f32[4,32,4,256]{3,2,1,0:T(4,128)}), f32[4,32,4,256]{3,2,1,0:T(4,128)S(1)}, u32[]{:S(2)}, u32[]{:S(2)}) async-start(f32[4,32,4,256]{3,2,1,0:T(4,128)} %bitcast.35), calls=%async_computation.8 | async-start | bytes 1048576 | tf_op jit(solution)/shard_map/all_to_all | solution.py:42
  48.8 8.0 %all-to-all-done.8 = f32[4,32,4,256]{3,2,1,0:T(4,128)S(1)} async-done(((f32[4,32,4,256]{3,2,1,0:T(4,128)}), f32[4,32,4,256]{3,2,1,0:T(4,128)S(1)}, u32[]{:S(2)}, u32[]{:S(2)}) %all-to-all-start.8) | async-done | bytes 524320 | tf_op jit(solution)/shard_map/all_to_all | solution.py:42
  56.9 13.8 %all_to_all.80 = f32[32,4,256]{2,1,0:T(4,128)S(1)} all-to-all(f32[32,4,256]{2,1,0:T(4,128)S(1)} %broadcast_in_dim.115), channel_id=1, replica_groups=mesh['rows_0'=8,'rows_1'=4,'rows_2'=4,'tgt'=2] {'rows_0','rows_1'}, dimensions={0} | all-to-all | bytes 262144 | tf_op jit(solution)/shard_map/all_to_all | solution.py:17
  71.5 3.5 %all-to-all-start.3 = ((f32[4,32,4,256]{3,2,1,0:T(4,128)}), f32[4,32,4,256]{3,2,1,0:T(4,128)S(1)}, u32[]{:S(2)}, u32[]{:S(2)}) async-start(f32[4,32,4,256]{3,2,1,0:T(4,128)} %broadcast_in_dim.116), calls=%async_computation.3 | async-start | bytes 1048576 | tf_op jit(solution)/shard_map/all_to_all | solution.py:17
  76.4 6.6 %all-to-all-done.3 = f32[4,32,4,256]{3,2,1,0:T(4,128)S(1)} async-done(((f32[4,32,4,256]{3,2,1,0:T(4,128)}), f32[4,32,4,256]{3,2,1,0:T(4,128)S(1)}, u32[]{:S(2)}, u32[]{:S(2)}) %all-to-all-start.3) | async-done | bytes 524320 | tf_op jit(solution)/shard_map/all_to_all | solution.py:17
  83.0 4.7 %all-to-all-start.9 = ((f32[32,4,256]{2,1,0:T(4,128)}), f32[32,4,256]{2,1,0:T(4,128)S(1)}, u32[]{:S(2)}, u32[]{:S(2)}) async-start(f32[32,4,256]{2,1,0:T(4,128)} %reduce_sum.76), calls=%async_computation.9 | async-start | bytes 262144 | tf_op jit(solution)/shard_map/all_to_all | solution.py:50
  92.3 22.5 %while.28 = (s32[]{:T(128)}, f32[2048,512]{1,0:T(8,128)}, f32[512,128]{1,0:T(8,128)S(1)}, s32[]{:T(128)}, s32[]{:T(128)}, /*index=5*/f32[2048,256]{1,0:T(8,128)S...) while((s32[]{:T(128)}, f32[2048,512]{1,0:T(8,128)}, ...), condition=%wide.region_3.5_spmd, body=%wide.region_2.4_spmd.sunk | while | flops 1209336832 | bytes 4982959 | solution.py:116
  95.2 2.8 convolution_add_fusion.4
  100.8 2.8 convolution_add_fusion.4
  106.4 2.8 convolution_add_fusion.4
  115.6 3.4 %all-to-all-start.4 = ((f32[4,32,4,128]{3,2,1,0:T(4,128)}), f32[4,32,4,128]{3,2,1,0:T(4,128)S(1)}, u32[]{:S(2)}, u32[]{:S(2)}) async-start(f32[4,32,4,128]{3,2,1,0:T(4,128)} %copy.29), calls=%async_computation.4 | async-start | bytes 524288 | tf_op jit(solution)/shard_map/all_to_all | solution.py:42
  119.0 6.6 %all-to-all-done.4 = f32[4,32,4,128]{3,2,1,0:T(4,128)S(1)} async-done(((f32[4,32,4,128]{3,2,1,0:T(4,128)}), f32[4,32,4,128]{3,2,1,0:T(4,128)S(1)}, u32[]{:S(2)}, u32[]{:S(2)}) %all-to-all-start.4) | async-done | bytes 262176 | tf_op jit(solution)/shard_map/all_to_all | solution.py:42
  126.3 8.6 %all-to-all-start.10 = ((f32[32,4,256]{2,1,0:T(4,128)}), f32[32,4,256]{2,1,0:T(4,128)S(1)}, u32[]{:S(2)}, u32[]{:S(2)}) async-start(f32[32,4,256]{2,1,0:T(4,128)} %broadcast_in_dim.120), calls=%async_computation.10 | async-start | bytes 262144 | tf_op jit(solution)/shard_map/all_to_all | solution.py:17
  135.0 9.5 %all-to-all-done.10 = f32[32,4,256]{2,1,0:T(4,128)S(1)} async-done(((f32[32,4,256]{2,1,0:T(4,128)}), f32[32,4,256]{2,1,0:T(4,128)S(1)}, u32[]{:S(2)}, u32[]{:S(2)}) %all-to-all-start.10) | async-done | bytes 131104 | tf_op jit(solution)/shard_map/all_to_all | solution.py:17
  144.5 13.2 %all_to_all.81 = f32[32,4,128]{2,1,0:T(4,128)S(1)} all-to-all(f32[32,4,128]{2,1,0:T(4,128)S(1)} %reduce_sum.74), channel_id=1, replica_groups=mesh['rows_0'=8,'rows_1'=4,'rows_2'=4,'tgt'=2] {'rows_0','rows_1'}, dimensions={0} | all-to-all | bytes 131072 | tf_op jit(solution)/shard_map/all_to_all | solution.py:50
  158.6 3.5 %all-to-all-start.11 = ((f32[4,32,4,256]{3,2,1,0:T(4,128)}), f32[4,32,4,256]{3,2,1,0:T(4,128)S(1)}, u32[]{:S(2)}, u32[]{:S(2)}) async-start(f32[4,32,4,256]{3,2,1,0:T(4,128)} %broadcast_in_dim.121), calls=%async_computation.11 | async-start | bytes 1048576 | tf_op jit(solution)/shard_map/all_to_all | solution.py:17
  162.1 8.0 %all-to-all-done.11 = f32[4,32,4,256]{3,2,1,0:T(4,128)S(1)} async-done(((f32[4,32,4,256]{3,2,1,0:T(4,128)}), f32[4,32,4,256]{3,2,1,0:T(4,128)S(1)}, u32[]{:S(2)}, u32[]{:S(2)}) %all-to-all-start.11) | async-done | bytes 524320 | tf_op jit(solution)/shard_map/all_to_all | solution.py:17
  170.1 13.1 %all_to_all.82 = f32[32,4,128]{2,1,0:T(4,128)S(1)} all-to-all(f32[32,4,128]{2,1,0:T(4,128)S(1)} %broadcast_in_dim.117), channel_id=1, replica_groups=mesh['rows_0'=8,'rows_1'=4,'rows_2'=4,'tgt'=2] {'rows_0','rows_1'}, dimensions={0} | all-to-all | bytes 131072 | tf_op jit(solution)/shard_map/all_to_all | solution.py:17
  184.0 3.6 %all-to-all-start.7 = ((f32[4,32,4,128]{3,2,1,0:T(4,128)}), f32[4,32,4,128]{3,2,1,0:T(4,128)S(1)}, u32[]{:S(2)}, u32[]{:S(2)}) async-start(f32[4,32,4,128]{3,2,1,0:T(4,128)} %broadcast_in_dim.118), calls=%async_computation.7 | async-start | bytes 524288 | tf_op jit(solution)/shard_map/all_to_all | solution.py:17
  187.8 6.2 %all-to-all-done.7 = f32[4,32,4,128]{3,2,1,0:T(4,128)S(1)} async-done(((f32[4,32,4,128]{3,2,1,0:T(4,128)}), f32[4,32,4,128]{3,2,1,0:T(4,128)S(1)}, u32[]{:S(2)}, u32[]{:S(2)}) %all-to-all-start.7) | async-done | bytes 262176 | tf_op jit(solution)/shard_map/all_to_all | solution.py:17
  196.5 6.9 %convolution_subtract_fusion.1 = f32[2048,128]{1,0:T(8,128)} fusion(f32[2048,128]{1,0:T(8,128)} %get-tuple-element.444, f32[2048,512]{1,0:T(8,128)} %get-tuple-element.216, f32[128,512]{1,0:T(8,128)S(1)} %fusion.14), kind=kOutput, calls=%fused_computation.25 | convolution fusion | flops 1610874880 | bytes 6553600 | tf_op jit(solution)/shard_map/dot_general | solution.py:124
  205.9 22.5 %while.29 = (s32[]{:T(128)}, f32[2048,512]{1,0:T(8,128)}, f32[512,128]{1,0:T(8,128)S(1)}, s32[]{:T(128)}, s32[]{:T(128)}, /*index=5*/f32[2048,256]{1,0:T(8,128)S...) while((s32[]{:T(128)}, f32[2048,512]{1,0:T(8,128)}, ...), condition=%wide.region_9.11_spmd, body=%wide.region_8.10_spmd.sunk | while | flops 1209336832 | bytes 4982959 | solution.py:116
  228.5 9.2 %all_to_all.85 = f32[4,32,4,128]{3,2,1,0:T(4,128)S(1)} all-to-all(f32[4,32,4,128]{3,2,1,0:T(4,128)S(1)} %copy.35), channel_id=1, replica_groups=mesh['rows_0'=8,'rows_1'=4,'rows_2'=4,'tgt'=2] {'rows_2'}, dimensions={0} | all-to-all | bytes 524288 | tf_op jit(solution)/shard_map/all_to_all | solution.py:42
  237.8 13.0 %all_to_all.86 = f32[32,4,128]{2,1,0:T(4,128)S(1)} all-to-all(f32[32,4,128]{2,1,0:T(4,128)S(1)} %reduce_sum.78), channel_id=1, replica_groups=mesh['rows_0'=8,'rows_1'=4,'rows_2'=4,'tgt'=2] {'rows_0','rows_1'}, dimensions={0} | all-to-all | bytes 131072 | tf_op jit(solution)/shard_map/all_to_all | solution.py:50
  250.8 13.1 %all_to_all.83 = f32[32,4,128]{2,1,0:T(4,128)S(1)} all-to-all(f32[32,4,128]{2,1,0:T(4,128)S(1)} %broadcast_in_dim.122), channel_id=1, replica_groups=mesh['rows_0'=8,'rows_1'=4,'rows_2'=4,'tgt'=2] {'rows_0','rows_1'}, dimensions={0} | all-to-all | bytes 131072 | tf_op jit(solution)/shard_map/all_to_all | solution.py:17
  263.9 9.1 %all_to_all.84 = f32[4,32,4,128]{3,2,1,0:T(4,128)S(1)} all-to-all(f32[4,32,4,128]{3,2,1,0:T(4,128)S(1)} %broadcast_in_dim.123), channel_id=1, replica_groups=mesh['rows_0'=8,'rows_1'=4,'rows_2'=4,'tgt'=2] {'rows_2'}, dimensions={0} | all-to-all | bytes 524288 | tf_op jit(solution)/shard_map/all_to_all | solution.py:17
  275.5 6.6 %convolution_subtract_fusion = f32[2048,128]{1,0:T(8,128)} fusion(f32[2048,128]{1,0:T(8,128)S(1)} %copy-done.1, f32[2048,512]{1,0:T(8,128)} %get-tuple-element.218, f32[128,512]{1,0:T(8,128)S(1)} %fusion.12), kind=kOutput, calls=%fused_computation.24 | convolution fusion | flops 1610874880 | bytes 6553600 | tf_op jit(solution)/shard_map/dot_general | solution.py:124
  (72 shorter events, 62.1 us)
Async XLA Ops:
  0.0 4.9 %copy-start = (f32[2048,256]{1,0:T(8,128)S(1)}, f32[2048,256]{1,0:T(8,128)}, u32[]{:S(2)}) copy-start(f32[2048,256]{1,0:T(8,128)} %param.12) | copy-start | bytes 6291460
  7.8 28.0 %copy-start.2 = (f32[512,256]{1,0:T(8,128)S(1)}, f32[512,256]{1,0:T(8,128)}, u32[]{:S(2)}) copy-start(f32[512,256]{1,0:T(8,128)} %get-tuple-element.260) | copy-start | bytes 1572868
  9.9 13.9 %all-to-all-start = ((f32[4,32,4,256]{3,2,1,0:T(4,128)}), f32[4,32,4,256]{3,2,1,0:T(4,128)S(1)}, u32[]{:S(2)}, u32[]{:S(2)}) async-start(f32[4,32,4,256]{3,2,1,0:T(4,128)} %bitcast.50), calls=%async_computation | async-start | bytes 1048576 | tf_op jit(solution)/shard_map/all_to_all | solution.py:42
  24.6 20.7 %all-to-all-start.1 = ((f32[32,4,256]{2,1,0:T(4,128)}), f32[32,4,256]{2,1,0:T(4,128)S(1)}, u32[]{:S(2)}, u32[]{:S(2)}) async-start(f32[32,4,256]{2,1,0:T(4,128)} %reduce_sum.72), calls=%async_computation.1 | async-start | bytes 262144 | tf_op jit(solution)/shard_map/all_to_all | solution.py:50
  45.3 11.5 %all-to-all-start.8 = ((f32[4,32,4,256]{3,2,1,0:T(4,128)}), f32[4,32,4,256]{3,2,1,0:T(4,128)S(1)}, u32[]{:S(2)}, u32[]{:S(2)}) async-start(f32[4,32,4,256]{3,2,1,0:T(4,128)} %bitcast.35), calls=%async_computation.8 | async-start | bytes 1048576 | tf_op jit(solution)/shard_map/all_to_all | solution.py:42
  71.5 11.5 %all-to-all-start.3 = ((f32[4,32,4,256]{3,2,1,0:T(4,128)}), f32[4,32,4,256]{3,2,1,0:T(4,128)S(1)}, u32[]{:S(2)}, u32[]{:S(2)}) async-start(f32[4,32,4,256]{3,2,1,0:T(4,128)} %broadcast_in_dim.116), calls=%async_computation.3 | async-start | bytes 1048576 | tf_op jit(solution)/shard_map/all_to_all | solution.py:17
  83.0 32.5 %all-to-all-start.9 = ((f32[32,4,256]{2,1,0:T(4,128)}), f32[32,4,256]{2,1,0:T(4,128)S(1)}, u32[]{:S(2)}, u32[]{:S(2)}) async-start(f32[32,4,256]{2,1,0:T(4,128)} %reduce_sum.76), calls=%async_computation.9 | async-start | bytes 262144 | tf_op jit(solution)/shard_map/all_to_all | solution.py:50
  115.6 10.1 %all-to-all-start.4 = ((f32[4,32,4,128]{3,2,1,0:T(4,128)}), f32[4,32,4,128]{3,2,1,0:T(4,128)S(1)}, u32[]{:S(2)}, u32[]{:S(2)}) async-start(f32[4,32,4,128]{3,2,1,0:T(4,128)} %copy.29), calls=%async_computation.4 | async-start | bytes 524288 | tf_op jit(solution)/shard_map/all_to_all | solution.py:42
  126.3 18.2 %all-to-all-start.10 = ((f32[32,4,256]{2,1,0:T(4,128)}), f32[32,4,256]{2,1,0:T(4,128)S(1)}, u32[]{:S(2)}, u32[]{:S(2)}) async-start(f32[32,4,256]{2,1,0:T(4,128)} %broadcast_in_dim.120), calls=%async_computation.10 | async-start | bytes 262144 | tf_op jit(solution)/shard_map/all_to_all | solution.py:17
  158.6 11.5 %all-to-all-start.11 = ((f32[4,32,4,256]{3,2,1,0:T(4,128)}), f32[4,32,4,256]{3,2,1,0:T(4,128)S(1)}, u32[]{:S(2)}, u32[]{:S(2)}) async-start(f32[4,32,4,256]{3,2,1,0:T(4,128)} %broadcast_in_dim.121), calls=%async_computation.11 | async-start | bytes 1048576 | tf_op jit(solution)/shard_map/all_to_all | solution.py:17
  184.0 10.1 %all-to-all-start.7 = ((f32[4,32,4,128]{3,2,1,0:T(4,128)}), f32[4,32,4,128]{3,2,1,0:T(4,128)S(1)}, u32[]{:S(2)}, u32[]{:S(2)}) async-start(f32[4,32,4,128]{3,2,1,0:T(4,128)} %broadcast_in_dim.118), calls=%async_computation.7 | async-start | bytes 524288 | tf_op jit(solution)/shard_map/all_to_all | solution.py:17
  228.4 47.1 %copy-start.1 = (f32[2048,128]{1,0:T(8,128)S(1)}, f32[2048,128]{1,0:T(8,128)}, u32[]{:S(2)}) copy-start(f32[2048,128]{1,0:T(8,128)} %get-tuple-element.443) | copy-start | bytes 3145732
where the time goes:
time: 284 us; the launch traced here: 282 us
  blocking collectives  84.4 us (30%)
  waiting for transfers between devices  63 us (22%)
  matrix products  57.9 us (20%)
  starting transfers between devices  46.4 us (16%)
  local copies, waits for them, and re-layouts  19.2 us (7%)
  other arithmetic  10 us (4%)
    all_to_all x4, blocking collectives, sent_to_all(): lax.all_to_all(jnp.broadcast_to(shard[None], (count, *shard.shape)), axis...  49 us
    all_to_all x4, waiting for transfers between devices, sent_to_all(): lax.all_to_all(jnp.broadcast_to(shard[None], (count, *shard.shape)), axis...  30.4 us
    all_to_all x2, blocking collectives, sum_in_two_steps(): lax.all_to_all(nearer, far, split_axis=0, concat_axis=0, tiled=True)  26.2 us
    all_to_all x3, waiting for transfers between devices, summed_on_arrival(): lax.all_to_all(pieces, axis, split_axis=0, concat_axis=0, tiled=True)  24.1 us
    dot_general x8, matrix products, accumulate(): lax.dot_general(columns, current, (((0,), (0,)), ((), ())), precision=lax...  22.3 us
    all_to_all x4, starting transfers between devices, sent_to_all(): lax.all_to_all(jnp.broadcast_to(shard[None], (count, *shard.shape)), axis...  19.2 us
    dot_general x8, matrix products, kernel_columns(): lax.dot_general(rows_in, points, (((1,), (1,)), ((), ())), precision=lax....  17.2 us
    all_to_all x2, starting transfers between devices, sum_in_two_steps(): lax.all_to_all(nearer, far, split_axis=0, concat_axis=0, tiled=True)  15.9 us
  transfers between devices with their start and end apart: 9, of which 8 were waited for; matrix products, arithmetic and copies ran while one was open for 11% of the time, Pallas kernels for 0%

commit v1 on v0

v1 whole, which is shorter than its diff:
```python
import functools

import jax
import jax.numpy as jnp
from jax import lax
from jax.experimental import pallas as pl
from jax.experimental.pallas import tpu as pltpu
from jax.sharding import Mesh
from jax.sharding import PartitionSpec as P

ROWS = ("rows_0", "rows_1", "rows_2")
MESH = pl.DeviceIdType.MESH
NZ, NX, NY = 8, 4, 4
PLANE = NX * NY
TILE = 256
NT = (((1,), (1,)), ((), ()))
NN = (((1,), (0,)), ((), ()))


def ring_hops(step, size):
    return min(step, size - step)


PLANE_STEPS = sorted(
    [(kx, ky) for kx in range(NX) for ky in range(NY) if (kx, ky) != (0, 0)],
    key=lambda k: -(ring_hops(k[0], NX) + ring_hops(k[1], NY)),
)
LINE_STEPS = sorted(range(1, NZ), key=lambda k: -ring_hops(k, NZ))


def halves(value):
    high = value.astype(jnp.bfloat16)
    low = (value - high.astype(jnp.float32)).astype(jnp.bfloat16)
    return high, low


def dot(left, right, dims):
    return lax.dot_general(left, right, dims, preferred_element_type=jnp.float32)


def kernel(
    counts, ids, samples, targets, inverse, out,
    x_high, x_low, r_turned, residual, p_high, p_low, c_high, c_low, b_high, b_low,
    p_part, p_in, p_line, p_line_in, p_full,
    s_part, s_in, s_line, s_line_in, k_full,
    send_sems, recv_sems,
):
    z, x, y = (lax.axis_index(name) for name in ROWS)
    core = lax.axis_index("tgt")
    place = x * NY + y
    other = 1 - core
    rows = samples.shape[0]
    block = ids.shape[1]
    blocks = ids.shape[0]
    mine = block // 2
    p_piece = mine // PLANE
    s_piece = targets.shape[1] // PLANE
    wide = targets.shape[1]
    tiles = rows // TILE

    def plane_peer(step):
        px, py = lax.rem(x + step[0], NX), lax.rem(y + step[1], NY)
        return (z, px, py, core), px * NY + py

    def line_peer(step):
        return (lax.rem(z + step, NZ), x, y, core)

    partner = (z, x, y, other)

    barrier = pltpu.get_barrier_semaphore()
    for step in PLANE_STEPS:
        pl.semaphore_signal(barrier, inc=1, device_id=plane_peer(step)[0], device_id_type=MESH)
    for step in LINE_STEPS:
        pl.semaphore_signal(barrier, inc=1, device_id=line_peer(step), device_id_type=MESH)
    pl.semaphore_signal(barrier, inc=1, device_id=partner, device_id_type=MESH)

    def remote(src, dst, stage, device):
        return pltpu.make_async_remote_copy(
            src_ref=src, dst_ref=dst, send_sem=send_sems.at[stage], recv_sem=recv_sems.at[stage],
            device_id=device, device_id_type=MESH,
        )

    def arrived(stage, ref):
        pltpu.make_async_copy(ref, ref, recv_sems.at[stage]).wait()

    def sent(stage, ref):
        pltpu.make_async_copy(ref, ref, send_sems.at[stage]).wait()

    def scatter_start(part, landing, size, stage):
        for slot, step in enumerate(PLANE_STEPS):
            device, index = plane_peer(step)
            start = pl.multiple_of(index * size, size)
            remote(part.at[pl.ds(start, size)], landing.at[slot], stage, device).start()

    def scatter_finish(part, landing, size, stage, line):
        arrived(stage, landing)
        total = part[pl.ds(pl.multiple_of(place * size, size), size)]
        for slot in range(PLANE - 1):
            total = total + landing[slot]
        line[...] = total

    def line_start(line, landing, stage):
        for slot, step in enumerate(LINE_STEPS):
            remote(line, landing.at[slot], stage, line_peer(step)).start()

    def line_finish(line, landing, stage):
        arrived(stage, landing)
        total = line[...]
        for slot in range(NZ - 1):
            total = total + landing[slot]
        return total

    def gather_start(full, start, size, stage):
        piece = full.at[pl.ds(start, size)]
        for step in PLANE_STEPS:
            remote(piece, piece, stage, plane_peer(step)[0]).start()

    def points_stage(b, n):
        return 5 * b + n

    def sums_stage(b, n):
        return 5 * blocks + 3 * b + n

    def split_samples(i, carry):
        at = pl.ds(pl.multiple_of(i * TILE, TILE), TILE)
        high, low = halves(samples[at])
        x_high[at] = high
        x_low[at] = low
        return carry

    lax.fori_loop(0, tiles, split_samples, 0)

    first = ((z * NX + x) * NY + y) * rows

    def pick(b):
        wanted = ids[pl.ds(b, 1), pl.ds(pl.multiple_of(core * mine, mine), mine)] - first
        column = jnp.broadcast_to(wanted.astype(jnp.float32), (8, mine)).T[:, :1]
        slots = lax.broadcasted_iota(jnp.int32, (mine, rows), 1).astype(jnp.float32)
        chosen = jnp.where(column == slots, 1.0, 0.0).astype(jnp.bfloat16)
        p_part[b] = dot(chosen, x_high[...], NN) + dot(chosen, x_low[...], NN)

    pick(0)
    pl.semaphore_wait(barrier, PLANE + NZ - 1)
    scatter_start(p_part.at[0], p_in.at[0], p_piece, points_stage(0, 0))
    pick(1)
    scatter_start(p_part.at[1], p_in.at[1], p_piece, points_stage(1, 0))

    def turn(value, i):
        at = pl.ds(pl.multiple_of(i * TILE, TILE), TILE)
        high, low = halves(value.T)
        r_turned[pl.ds(0, wide), at] = high
        r_turned[pl.ds(wide, wide), at] = low

    def turn_targets(i, carry):
        turn(targets[pl.ds(pl.multiple_of(i * TILE, TILE), TILE)], i)
        return carry

    lax.fori_loop(0, tiles, turn_targets, 0)
    for b in range(blocks):
        b_high[b], b_low[b] = halves(inverse[b])

    for b in range(blocks):
        scatter_finish(p_part.at[b], p_in.at[b], p_piece, points_stage(b, 0), p_line.at[b])
        line_start(p_line.at[b], p_line_in.at[b], points_stage(b, 1))
    own = pl.multiple_of(core * mine, mine)
    own_piece = pl.multiple_of(core * mine + place * p_piece, p_piece)
    for b in range(blocks):
        total = line_finish(p_line.at[b], p_line_in.at[b], points_stage(b, 1))
        p_full[b, pl.ds(own_piece, p_piece)] = total
        gather_start(p_full.at[b], own_piece, p_piece, points_stage(b, 2))

    def swap_halves(b):
        arrived(points_stage(b, 2), p_in.at[b])
        half = p_full.at[b, pl.ds(own, mine)]
        remote(half, half, points_stage(b, 3), partner).start()

    def points_ready(b):
        arrived(points_stage(b, 3), p_part.at[b])
        p_high[b], p_low[b] = halves(p_full[b] * (0.5 / samples.shape[1] ** 0.5))

    live = counts[0]

    def columns_tile(b, i):
        at = pl.ds(pl.multiple_of(i * TILE, TILE), TILE)
        near = (
            dot(x_high[at], p_high[b], NT)
            + dot(x_high[at], p_low[b], NT)
            + dot(x_low[at], p_high[b], NT)
        ) + 1.0
        slots = i * TILE + lax.broadcasted_iota(jnp.int32, near.shape, 0)
        high, low = halves(jnp.where(slots < live, near * near * near, 0.0))
        c_high[b, at] = high
        c_low[b, at] = low
        return high, low

    def add_sums(b, i, high, low):
        across = pl.ds(pl.multiple_of(i * TILE, TILE), TILE)
        both = dot(r_turned[:, across], high, NN)
        s_part[b] += both[:wide] + both[wide:] + dot(r_turned[pl.ds(0, wide), across], low, NN)

    def update(b, i, current):
        at = pl.ds(pl.multiple_of(i * TILE, TILE), TILE)
        coefs = k_full[b]
        c_h, c_l = halves(coefs)
        both = dot(c_high[b, at], jnp.concatenate([c_h, c_l], axis=0), NT)
        return current - (both[:, :wide] + both[:, wide:] + dot(c_low[b, at], c_h, NT))

    def sums_exchange(b):
        scatter_finish(s_part.at[b], s_in.at[b], s_piece, sums_stage(b, 0), s_line.at[b])
        line_start(s_line.at[b], s_line_in.at[b], sums_stage(b, 1))
        sums = line_finish(s_line.at[b], s_line_in.at[b], sums_stage(b, 1))
        high, low = halves(sums)
        at = pl.multiple_of(place * s_piece, s_piece)
        k_full[b, pl.ds(at, s_piece)] = (
            dot(high, b_high[b], NT) + dot(high, b_low[b], NT) + dot(low, b_high[b], NT)
        )
        gather_start(k_full.at[b], at, s_piece, sums_stage(b, 2))
        arrived(sums_stage(b, 2), s_in.at[b])

    swap_halves(0)
    points_ready(0)
    s_part[...] = jnp.zeros_like(s_part)

    def first_block(i, carry):
        add_sums(0, i, *columns_tile(0, i))
        return carry

    lax.fori_loop(0, tiles, first_block, 0)
    scatter_start(s_part.at[0], s_in.at[0], s_piece, sums_stage(0, 0))
    swap_halves(1)
    points_ready(1)

    def second_columns(i, carry):
        columns_tile(1, i)
        return carry

    lax.fori_loop(0, tiles, second_columns, 0)
    sums_exchange(0)

    def second_block(i, carry):
        at = pl.ds(pl.multiple_of(i * TILE, TILE), TILE)
        left = update(0, i, targets[at])
        residual[at] = left
        turn(left, i)
        add_sums(1, i, c_high[1, at], c_low[1, at])
        return carry

    lax.fori_loop(0, tiles, second_block, 0)
    scatter_start(s_part.at[1], s_in.at[1], s_piece, sums_stage(1, 0))
    sums_exchange(1)

    def last(i, carry):
        at = pl.ds(pl.multiple_of(i * TILE, TILE), TILE)
        out[at] = update(1, i, residual[at])
        return carry

    lax.fori_loop(0, tiles, last, 0)

    for b in range(blocks):
        sent(points_stage(b, 0), p_in.at[b])
        sent(points_stage(b, 1), p_line_in.at[b])
        sent(points_stage(b, 2), p_in.at[b])
        sent(points_stage(b, 3), p_part.at[b])
        sent(sums_stage(b, 0), s_in.at[b])
        sent(sums_stage(b, 1), s_line_in.at[b])
        sent(sums_stage(b, 2), s_in.at[b])


def on_device(counts, samples, targets, point_ids, block_inverse):
    rows, feat = samples.shape
    blocks, block = point_ids.shape
    wide = targets.shape[1]
    mine = block // 2
    p_piece, s_piece = mine // PLANE, wide // PLANE
    f32, bf16 = jnp.float32, jnp.bfloat16
    vmem = pl.BlockSpec(memory_space=pltpu.VMEM)
    return pl.pallas_call(
        kernel,
        out_shape=jax.ShapeDtypeStruct(targets.shape, f32),
        in_specs=[pl.BlockSpec(memory_space=pltpu.SMEM), vmem, vmem, vmem, vmem],
        out_specs=vmem,
        scratch_shapes=[
            pltpu.VMEM((rows, feat), bf16),
            pltpu.VMEM((rows, feat), bf16),
            pltpu.VMEM((2 * wide, rows), bf16),
            pltpu.VMEM((rows, wide), f32),
            pltpu.VMEM((blocks, block, feat), bf16),
            pltpu.VMEM((blocks, block, feat), bf16),
            pltpu.VMEM((blocks, rows, block), bf16),
            pltpu.VMEM((blocks, rows, block), bf16),
            pltpu.VMEM((blocks, block, block), bf16),
            pltpu.VMEM((blocks, block, block), bf16),
            pltpu.VMEM((blocks, mine, feat), f32),
            pltpu.VMEM((blocks, PLANE - 1, p_piece, feat), f32),
            pltpu.VMEM((blocks, p_piece, feat), f32),
            pltpu.VMEM((blocks, NZ - 1, p_piece, feat), f32),
            pltpu.VMEM((blocks, block, feat), f32),
            pltpu.VMEM((blocks, wide, block), f32),
            pltpu.VMEM((blocks, PLANE - 1, s_piece, block), f32),
            pltpu.VMEM((blocks, s_piece, block), f32),
            pltpu.VMEM((blocks, NZ - 1, s_piece, block), f32),
            pltpu.VMEM((blocks, wide, block), f32),
            pltpu.SemaphoreType.DMA((8 * blocks,)),
            pltpu.SemaphoreType.DMA((8 * blocks,)),
        ],
        compiler_params=pltpu.CompilerParams(collective_id=0, has_side_effects=True),
    )(counts, point_ids, samples, targets, block_inverse)


def solution(mesh):
    finer = Mesh(
        mesh.devices.reshape(NZ, NX, NY, mesh.shape["tgt"]), ("rows_0", "rows_1", "rows_2", "tgt")
    )
    placed = (P(ROWS), P(ROWS, None), P(ROWS, "tgt"), P(), P())
    return jax.shard_map(
        on_device, mesh=finer, in_specs=placed, out_specs=P(ROWS, "tgt"), check_vma=False
    )
```

time: 284 us -> 80.9 us (0.28)
  blocking collectives: 84.4 us -> 0 us
  Pallas kernels: 0 us -> 77.8 us
  waiting for transfers between devices: 63 us -> 0 us
  matrix products: 57.9 us -> 0 us
  starting transfers between devices: 46.4 us -> 0 us
  local copies, waits for them, and re-layouts: 19.2 us -> 2.26 us
  other arithmetic: 10 us -> 0 us
    all_to_all x7 -> x0, blocking collectives: 84.4 us -> none  [the longest x4 49 us: sent_to_all(): lax.all_to_all(jnp.broadcast_to(shard[None], (count, *shard.shape)), axis...]
    pallas_call x0 -> x1, Pallas kernels: none -> 77.8 us  [on_device(): pl.pallas_call(kernel, out_shape=jax.ShapeDtypeStruct(targets.shape, f32)...]
    all_to_all x9 -> x0, waiting for transfers between devices: 63 us -> none  [the longest x4 30.4 us: sent_to_all(): lax.all_to_all(jnp.broadcast_to(shard[None], (count, *shard.shape)), axis...]
    dot_general x20 -> x0, matrix products: 57.9 us -> none  [the longest x8 22.3 us: accumulate(): lax.dot_general(columns, current, (((0,), (0,)), ((), ())), precision=lax...]
    all_to_all x9 -> x0, starting transfers between devices: 46.4 us -> none  [the longest x4 19.2 us: sent_to_all(): lax.all_to_all(jnp.broadcast_to(shard[None], (count, *shard.shape)), axis...]
    another operation x10 -> x0, local copies, waits for them, and re-layouts: 9.41 us -> none
    lt x8 -> x0, other arithmetic: 5.23 us -> none  [accumulate(): slot_ids < live_count]
    gather x2 -> x0, local copies, waits for them, and re-layouts: 4.73 us -> none  [pick_rows(): taken = jnp.take(samples, jnp.clip(local, 0, rows_here - 1), axis=0)]
  transfers between devices with their start and end apart: 9 -> 0, of which waited for: 8 -> 0; matrix products, arithmetic and copies ran while one was open for 11% -> 0% of each run, Pallas kernels for 0% -> 0%
where the time goes in v1:
time: 80.9 us; the launch traced here: 80.8 us
  Pallas kernels  77.8 us (96%)
  local copies, waits for them, and re-layouts  2.26 us (3%)
    pallas_call x1, Pallas kernels, on_device(): pl.pallas_call(kernel, out_shape=jax.ShapeDtypeStruct(targets.shape, f32)...  77.8 us
    unnamed x1, local copies, waits for them, and re-layouts  2.26 us

profile of v1, /device:TPU:32, one launch (start us, length us, event | category | flops | bytes accessed | tf_op | source)
XLA Modules:
  0.0 80.8 jit_solution(12074111949656390447)
XLA Ops:
  0.7 77.8 %shard_map.55 = f32[2048,128]{1,0:T(8,128)} custom-call(s32[1]{0:T(128)S(6)} %copy.7.counts, s32[2,512]{1,0:T(2,128)} %ids.1, f32[2048,256]{1,0:T(8,128)} %samples.1, f32[2048,128]{1,0:T(8,128)} %targets.1, f32[2,512,512]{2,1,0:T(8,128)} %inverse.1), custom_call_target="tpu_custom_call" | custom-call | tf_op jit(solution)/shard_map/pallas_call | solution.py:277
  78.5 2.3 %copy.8 = f32[2048,128]{1,0:T(8,128)} copy(f32[2048,128]{1,0:T(8,128)} %shard_map.55) | data formatting | bytes 2097152

commit v2 on v1

v2 whole, which is shorter than its diff:
```python
import jax
import jax.numpy as jnp
from jax import lax
from jax.experimental import pallas as pl
from jax.experimental.pallas import tpu as pltpu
from jax.sharding import Mesh
from jax.sharding import PartitionSpec as P

ROWS = ("rows_0", "rows_1", "rows_2")
MESH = pl.DeviceIdType.MESH
NZ, NX, NY = 8, 4, 4
PLANE = NX * NY
TILE = 256
CHUNKS = 4
FIRST, SECOND = 2, 6
NT = (((1,), (1,)), ((), ()))
NN = (((1,), (0,)), ((), ()))
f32, bf16 = jnp.float32, jnp.bfloat16


def ring_hops(step, size):
    return min(step, size - step)


PLANE_STEPS = sorted(
    [(kx, ky) for kx in range(NX) for ky in range(NY) if (kx, ky) != (0, 0)],
    key=lambda k: -(ring_hops(k[0], NX) + ring_hops(k[1], NY)),
)
LINE_STEPS = sorted(range(1, NZ), key=lambda k: -ring_hops(k, NZ))


def halves(value):
    high = value.astype(bf16)
    low = (value - high.astype(f32)).astype(bf16)
    return high, low


def dot(left, right, dims):
    return lax.dot_general(left, right, dims, preferred_element_type=f32)


def tile_at(i):
    return pl.ds(pl.multiple_of(i * TILE, TILE), TILE)


def kernel(
    counts, ids_in, samples_in, targets_in, inverse_in, out,
    ids, samples, targets, inverse,
    x_high, x_low, r_turned, residual, p_high, p_low, c_high, c_low, b_high, b_low,
    cross, cross_high, cross_low,
    part, landing, line, line_in, full, swapped,
    in_sems, send_sems, recv_sems,
):
    z, x, y = (lax.axis_index(name) for name in ROWS)
    core = lax.axis_index("tgt")
    place = x * NY + y
    rows = samples.shape[0]
    tiles = rows // TILE
    blocks, block = ids.shape
    mine = block // 2
    unit = part.shape[1]
    piece = unit // PLANE
    wide = targets.shape[1]

    def plane_peer(step):
        px, py = lax.rem(x + step[0], NX), lax.rem(y + step[1], NY)
        return (z, px, py, core), px * NY + py

    def line_peer(step):
        return (lax.rem(z + step, NZ), x, y, core)

    partner = (z, x, y, 1 - core)

    barrier = pltpu.get_barrier_semaphore()
    for step in PLANE_STEPS:
        pl.semaphore_signal(barrier, inc=1, device_id=plane_peer(step)[0], device_id_type=MESH)
    for step in LINE_STEPS:
        pl.semaphore_signal(barrier, inc=1, device_id=line_peer(step), device_id_type=MESH)
    pl.semaphore_signal(barrier, inc=1, device_id=partner, device_id_type=MESH)

    chunk = rows // CHUNKS
    ids_copy = pltpu.make_async_copy(ids_in, ids, in_sems.at[CHUNKS])
    targets_copy = pltpu.make_async_copy(targets_in, targets, in_sems.at[CHUNKS + 1])
    inverse_copy = pltpu.make_async_copy(inverse_in, inverse, in_sems.at[CHUNKS + 2])

    def samples_copy(n):
        at = pl.ds(n * chunk, chunk)
        return pltpu.make_async_copy(samples_in.at[at], samples.at[at], in_sems.at[n])

    ids_copy.start()
    for n in range(CHUNKS):
        samples_copy(n).start()

    def remote(src, dst, stage, device):
        return pltpu.make_async_remote_copy(
            src_ref=src, dst_ref=dst, send_sem=send_sems.at[stage], recv_sem=recv_sems.at[stage],
            device_id=device, device_id_type=MESH,
        )

    def arrived(u, n, ref):
        pltpu.make_async_copy(ref, ref, recv_sems.at[4 * u + n]).wait()

    def sent(u, n, ref):
        pltpu.make_async_copy(ref, ref, send_sems.at[4 * u + n]).wait()

    own_piece = pl.ds(pl.multiple_of(place * piece, piece), piece)

    def scatter(u):
        for slot, step in enumerate(PLANE_STEPS):
            device, index = plane_peer(step)
            src = part.at[u, pl.ds(pl.multiple_of(index * piece, piece), piece)]
            remote(src, landing.at[u, slot], 4 * u, device).start()

    def to_line(u):
        arrived(u, 0, landing.at[u])
        total = part[u, own_piece]
        for slot in range(PLANE - 1):
            total = total + landing[u, slot]
        line[u] = total
        for slot, step in enumerate(LINE_STEPS):
            remote(line.at[u], line_in.at[u, slot], 4 * u + 1, line_peer(step)).start()

    def off_line(u):
        arrived(u, 1, line_in.at[u])
        total = line[u]
        for slot in range(NZ - 1):
            total = total + line_in[u, slot]
        return total

    def gather(u, value):
        full[u, own_piece] = value
        ref = full.at[u, own_piece]
        for step in PLANE_STEPS:
            remote(ref, ref, 4 * u + 2, plane_peer(step)[0]).start()

    def gathered(u):
        arrived(u, 2, landing.at[u])

    def swap(u):
        gathered(u)
        remote(full.at[u], swapped.at[u], 4 * u + 3, partner).start()

    per_chunk = tiles // CHUNKS
    for n in range(CHUNKS):
        samples_copy(n).wait()

        def split_samples(i, carry):
            at = tile_at(i)
            x_high[at], x_low[at] = halves(samples[at])
            return carry

        lax.fori_loop(n * per_chunk, (n + 1) * per_chunk, split_samples, 0)
    targets_copy.start()
    inverse_copy.start()
    ids_copy.wait()

    first = ((z * NX + x) * NY + y) * rows

    def pick(u):
        start = pl.multiple_of(core * mine + (u % 2) * unit, unit)
        wanted = ids[pl.ds(u // 2, 1), pl.ds(start, unit)] - first
        column = jnp.broadcast_to(wanted.astype(f32), (8, unit)).T[:, :1]
        slots = lax.broadcasted_iota(jnp.int32, (unit, rows), 1).astype(f32)
        chosen = jnp.where(column == slots, 1.0, 0.0).astype(bf16)
        part[u] = dot(chosen, x_high[...], NN) + dot(chosen, x_low[...], NN)

    pick(0)
    pl.semaphore_wait(barrier, PLANE + NZ - 1)
    scatter(0)
    pick(1)
    scatter(1)
    pick(2)
    pick(3)

    targets_copy.wait()

    def turn_targets(i, carry):
        at = tile_at(i)
        high, low = halves(targets[at].T)
        r_turned[pl.ds(0, wide), at] = high
        r_turned[pl.ds(wide, wide), at] = low
        return carry

    lax.fori_loop(0, tiles, turn_targets, 0)
    to_line(0)
    to_line(1)
    scatter(2)
    scatter(3)

    inverse_copy.wait()
    for b in range(blocks):
        for i in range(2):
            for j in range(2):
                from_i = pl.ds(pl.multiple_of((core + i) % 2 * mine, mine), mine)
                from_j = pl.ds(pl.multiple_of((core + j) % 2 * mine, mine), mine)
                high, low = halves(inverse[b, from_i, from_j])
                b_high[b, pl.ds(i * mine, mine), pl.ds(j * mine, mine)] = high
                b_low[b, pl.ds(i * mine, mine), pl.ds(j * mine, mine)] = low

    gather(0, off_line(0))
    gather(1, off_line(1))
    to_line(2)
    to_line(3)

    scale = 0.5 / samples.shape[1] ** 0.5

    def points_ready(b, h):
        for n in range(2):
            u = 2 * b + n
            if h == 1:
                arrived(u, 3, swapped.at[u])
            value = swapped[u] if h == 1 else full[u]
            at = pl.ds(h * mine + n * unit, unit)
            p_high[b, at], p_low[b, at] = halves(value * scale)

    live = counts[0]

    def columns_tile(b, h, i):
        at = tile_at(i)
        points = pl.ds(h * mine, mine)
        high, low = p_high[b, points], p_low[b, points]
        near = (dot(x_high[at], high, NT) + dot(x_high[at], low, NT) + dot(x_low[at], high, NT)) + 1.0
        slots = i * TILE + lax.broadcasted_iota(jnp.int32, near.shape, 0)
        cubed = jnp.where(slots < live, near * near * near, 0.0)
        high, low = halves(cubed)
        c_high[b, at, points] = high
        c_low[b, at, points] = low
        return cubed, high, low

    def add_sums(u, i, high, low):
        across = tile_at(i)
        both = dot(r_turned[:, across], high, NN)
        part[u] += both[:wide] + both[wide:] + dot(r_turned[pl.ds(0, wide), across], low, NN)

    def update(u, i, current):
        b, h = u // 2 - blocks, u % 2
        points = pl.ds(h * mine, mine)
        high, low = halves(full[u])
        both = dot(c_high[b, tile_at(i), points], jnp.concatenate([high, low], axis=0), NT)
        return current - (both[:, :wide] + both[:, wide:] + dot(c_low[b, tile_at(i), points], high, NT))

    def coefs(b):
        first_unit = 2 * (blocks + b)
        sums = jnp.concatenate([off_line(first_unit), off_line(first_unit + 1)], axis=1)
        high, low = halves(sums)
        both = jnp.concatenate([high, low], axis=0)
        for h in range(2):
            at = pl.ds(h * mine, mine)
            value = dot(both, b_high[b, at], NT)
            gather(first_unit + h, value[:piece] + value[piece:] + dot(high, b_low[b, at], NT))

    for u in range(2 * blocks, 4 * blocks):
        part[u] = jnp.zeros_like(part[u])
    cross[...] = jnp.zeros_like(cross)

    swap(0)
    swap(1)
    points_ready(0, 0)
    gather(2, off_line(2))
    gather(3, off_line(3))

    for h in range(2):
        if h == 1:
            points_ready(0, 1)

        def first_block(i, carry):
            cubed, high, low = columns_tile(0, h, i)
            add_sums(4 + h, i, high, low)
            return carry

        lax.fori_loop(0, tiles, first_block, 0)
        scatter(4 + h)

    swap(2)
    swap(3)
    points_ready(1, 0)
    to_line(4)
    points_ready(1, 1)

    def second_columns(i, carry):
        at = tile_at(i)
        for h in range(2):
            cubed, high, low = columns_tile(1, h, i)
            add_sums(6 + h, i, high, low)
            t_high, t_low = halves(cubed.T)
            cross[pl.ds(h * mine, mine)] += (
                dot(t_high, c_high[0, at], NN) + dot(t_high, c_low[0, at], NN) + dot(t_low, c_high[0, at], NN)
            )
        return carry

    lax.fori_loop(0, FIRST, second_columns, 0)
    to_line(5)
    lax.fori_loop(FIRST, SECOND, second_columns, 0)
    coefs(0)
    lax.fori_loop(SECOND, tiles, second_columns, 0)
    cross_high[...], cross_low[...] = halves(cross[...])

    gathered(4)
    gathered(5)
    high, low = halves(jnp.concatenate([full[4], full[5]], axis=1))
    both = jnp.concatenate([high, low], axis=0)
    for h in range(2):
        at = pl.ds(h * mine, mine)
        value = dot(both, cross_high[at], NT)
        part[6 + h] -= value[:wide] + value[wide:] + dot(high, cross_low[at], NT)
        scatter(6 + h)

    def first_update(i, carry):
        at = tile_at(i)
        residual[at] = update(5, i, update(4, i, targets[at]))
        return carry

    lax.fori_loop(0, tiles, first_update, 0)
    to_line(6)
    to_line(7)
    coefs(1)
    gathered(6)

    def second_update(i, carry):
        at = tile_at(i)
        residual[at] = update(6, i, residual[at])
        return carry

    lax.fori_loop(0, tiles, second_update, 0)
    gathered(7)

    def last_update(i, carry):
        at = tile_at(i)
        out[at] = update(7, i, residual[at])
        return carry

    lax.fori_loop(0, tiles, last_update, 0)

    for u in range(4 * blocks):
        sent(u, 0, landing.at[u])
        sent(u, 1, line_in.at[u])
        sent(u, 2, landing.at[u])
        if u < 2 * blocks:
            sent(u, 3, swapped.at[u])


def on_device(counts, samples, targets, point_ids, block_inverse):
    rows, feat = samples.shape
    blocks, block = point_ids.shape
    wide = targets.shape[1]
    units, unit, lanes = 4 * blocks, block // 4, block // 2
    piece = unit // PLANE
    anywhere = pl.BlockSpec(memory_space=pl.ANY)
    return pl.pallas_call(
        kernel,
        out_shape=jax.ShapeDtypeStruct(targets.shape, f32),
        in_specs=[pl.BlockSpec(memory_space=pltpu.SMEM)] + [anywhere] * 4,
        out_specs=pl.BlockSpec(memory_space=pltpu.VMEM),
        scratch_shapes=[
            pltpu.VMEM(point_ids.shape, jnp.int32),
            pltpu.VMEM((rows, feat), f32),
            pltpu.VMEM((rows, wide), f32),
            pltpu.VMEM((blocks, block, block), f32),
            pltpu.VMEM((rows, feat), bf16),
            pltpu.VMEM((rows, feat), bf16),
            pltpu.VMEM((2 * wide, rows), bf16),
            pltpu.VMEM((rows, wide), f32),
            pltpu.VMEM((blocks, block, feat), bf16),
            pltpu.VMEM((blocks, block, feat), bf16),
            pltpu.VMEM((blocks, rows, block), bf16),
            pltpu.VMEM((blocks, rows, block), bf16),
            pltpu.VMEM((blocks, block, block), bf16),
            pltpu.VMEM((blocks, block, block), bf16),
            pltpu.VMEM((block, block), f32),
            pltpu.VMEM((block, block), bf16),
            pltpu.VMEM((block, block), bf16),
            pltpu.VMEM((units, unit, lanes), f32),
            pltpu.VMEM((units, PLANE - 1, piece, lanes), f32),
            pltpu.VMEM((units, piece, lanes), f32),
            pltpu.VMEM((units, NZ - 1, piece, lanes), f32),
            pltpu.VMEM((units, unit, lanes), f32),
            pltpu.VMEM((2 * blocks, unit, lanes), f32),
            pltpu.SemaphoreType.DMA((CHUNKS + 3,)),
            pltpu.SemaphoreType.DMA((4 * units,)),
            pltpu.SemaphoreType.DMA((4 * units,)),
        ],
        compiler_params=pltpu.CompilerParams(collective_id=0, has_side_effects=True),
    )(counts, point_ids, samples, targets, block_inverse)


def solution(mesh):
    finer = Mesh(
        mesh.devices.reshape(NZ, NX, NY, mesh.shape["tgt"]), ("rows_0", "rows_1", "rows_2", "tgt")
    )
    placed = (P(ROWS), P(ROWS, None), P(ROWS, "tgt"), P(), P())
    return jax.shard_map(
        on_device, mesh=finer, in_specs=placed, out_specs=P(ROWS, "tgt"), check_vma=False
    )
```

time: 80.9 us -> 76.4 us (0.944)
  Pallas kernels: 77.8 us -> 73.3 us
    pallas_call x1, Pallas kernels: 77.8 us -> 73.3 us  [on_device(): pl.pallas_call(kernel, out_shape=jax.ShapeDtypeStruct(targets.shape, f32)...]
where the time goes in v2:
time: 76.4 us; the launch traced here: 76.2 us
  Pallas kernels  73.3 us (96%)
  local copies, waits for them, and re-layouts  2.26 us (3%)
    pallas_call x1, Pallas kernels, on_device(): pl.pallas_call(kernel, out_shape=jax.ShapeDtypeStruct(targets.shape, f32)...  73.3 us
    unnamed x1, local copies, waits for them, and re-layouts  2.26 us

profile of v2, /device:TPU:32, one launch (start us, length us, event | category | flops | bytes accessed | tf_op | source)
XLA Modules:
  0.0 76.2 jit_solution(15022828472897408252)
XLA Ops:
  0.7 73.3 %shard_map.55 = f32[2048,128]{1,0:T(8,128)} custom-call(s32[1]{0:T(128)S(6)} %copy.7.counts, s32[2,512]{1,0:T(2,128)} %ids_in.1, f32[2048,256]{1,0:T(8,128)} %samples_in.1, f32[2048,128]{1,0:T(8,128)} %targets_in.1, f32[2,512,512]{2,1,0:T(8,128)} %inverse_in.1), custom_call_target="tpu_custom_call" | custom-call | tf_op jit(solution)/shard_map/pallas_call | solution.py:349
  74.0 2.3 %copy.8 = f32[2048,128]{1,0:T(8,128)} copy(f32[2048,128]{1,0:T(8,128)} %shard_map.55) | data formatting | bytes 2097152

commit v3 on v2

--- a/solution.py
+++ b/solution.py
@@ -12,7 +12,6 @@
 PLANE = NX * NY
 TILE = 256
 CHUNKS = 4
-FIRST, SECOND = 2, 6
 NT = (((1,), (1,)), ((), ()))
 NN = (((1,), (0,)), ((), ()))
 f32, bf16 = jnp.float32, jnp.bfloat16
@@ -40,14 +39,14 @@
 
 
 def tile_at(i):
-    return pl.ds(pl.multiple_of(i * TILE, TILE), TILE)
+    return pl.ds(i * TILE if isinstance(i, int) else pl.multiple_of(i * TILE, TILE), TILE)
 
 
 def kernel(
     counts, ids_in, samples_in, targets_in, inverse_in, out,
     ids, samples, targets, inverse,
     x_high, x_low, r_turned, residual, p_high, p_low, c_high, c_low, b_high, b_low,
-    cross, cross_high, cross_low,
+    turned_high, turned_low, cross_high, cross_low,
     part, landing, line, line_in, full, swapped,
     in_sems, send_sems, recv_sems,
 ):
@@ -215,22 +214,20 @@
 
     live = counts[0]
 
-    def columns_tile(b, h, i):
-        at = tile_at(i)
-        points = pl.ds(h * mine, mine)
+    def columns(b, h, i):
+        at, points = tile_at(i), pl.ds(h * mine, mine)
         high, low = p_high[b, points], p_low[b, points]
         near = (dot(x_high[at], high, NT) + dot(x_high[at], low, NT) + dot(x_low[at], high, NT)) + 1.0
         slots = i * TILE + lax.broadcasted_iota(jnp.int32, near.shape, 0)
         cubed = jnp.where(slots < live, near * near * near, 0.0)
-        high, low = halves(cubed)
-        c_high[b, at, points] = high
-        c_low[b, at, points] = low
-        return cubed, high, low
-
-    def add_sums(u, i, high, low):
-        across = tile_at(i)
-        both = dot(r_turned[:, across], high, NN)
-        part[u] += both[:wide] + both[wide:] + dot(r_turned[pl.ds(0, wide), across], low, NN)
+        c_high[b, at, points], c_low[b, at, points] = halves(cubed)
+        return cubed
+
+    def sums(b, h):
+        points = pl.ds(h * mine, mine)
+        both = dot(r_turned[...], c_high[b, :, points], NN)
+        value = both[:wide] + both[wide:] + dot(r_turned[pl.ds(0, wide)], c_low[b, :, points], NN)
+        part[2 * (blocks + b) + h] = value
 
     def update(u, i, current):
         b, h = u // 2 - blocks, u % 2
@@ -249,10 +246,6 @@
             value = dot(both, b_high[b, at], NT)
             gather(first_unit + h, value[:piece] + value[piece:] + dot(high, b_low[b, at], NT))
 
-    for u in range(2 * blocks, 4 * blocks):
-        part[u] = jnp.zeros_like(part[u])
-    cross[...] = jnp.zeros_like(cross)
-
     swap(0)
     swap(1)
     points_ready(0, 0)
@@ -262,38 +255,31 @@
     for h in range(2):
         if h == 1:
             points_ready(0, 1)
-
-        def first_block(i, carry):
-            cubed, high, low = columns_tile(0, h, i)
-            add_sums(4 + h, i, high, low)
-            return carry
-
-        lax.fori_loop(0, tiles, first_block, 0)
+        for i in range(tiles):
+            columns(0, h, i)
+        sums(0, h)
         scatter(4 + h)
 
     swap(2)
     swap(3)
-    points_ready(1, 0)
+    for h in range(2):
+        points_ready(1, h)
+        for i in range(tiles):
+            high, low = halves(columns(1, h, i).T)
+            turned_high[pl.ds(h * mine, mine), tile_at(i)] = high
+            turned_low[pl.ds(h * mine, mine), tile_at(i)] = low
     to_line(4)
-    points_ready(1, 1)
-
-    def second_columns(i, carry):
-        at = tile_at(i)
-        for h in range(2):
-            cubed, high, low = columns_tile(1, h, i)
-            add_sums(6 + h, i, high, low)
-            t_high, t_low = halves(cubed.T)
-            cross[pl.ds(h * mine, mine)] += (
-                dot(t_high, c_high[0, at], NN) + dot(t_high, c_low[0, at], NN) + dot(t_low, c_high[0, at], NN)
-            )
-        return carry
-
-    lax.fori_loop(0, FIRST, second_columns, 0)
     to_line(5)
-    lax.fori_loop(FIRST, SECOND, second_columns, 0)
+    for h in range(2):
+        at = pl.ds(h * mine, mine)
+        sums(1, h)
+        value = (
+            dot(turned_high[at], c_high[0], NN)
+            + dot(turned_high[at], c_low[0], NN)
+            + dot(turned_low[at], c_high[0], NN)
+        )
+        cross_high[at], cross_low[at] = halves(value)
     coefs(0)
-    lax.fori_loop(SECOND, tiles, second_columns, 0)
-    cross_high[...], cross_low[...] = halves(cross[...])
 
     gathered(4)
     gathered(5)
@@ -305,31 +291,20 @@
         part[6 + h] -= value[:wide] + value[wide:] + dot(high, cross_low[at], NT)
         scatter(6 + h)
 
-    def first_update(i, carry):
+    for i in range(tiles):
         at = tile_at(i)
         residual[at] = update(5, i, update(4, i, targets[at]))
-        return carry
-
-    lax.fori_loop(0, tiles, first_update, 0)
     to_line(6)
     to_line(7)
     coefs(1)
     gathered(6)
-
-    def second_update(i, carry):
+    for i in range(tiles):
         at = tile_at(i)
         residual[at] = update(6, i, residual[at])
-        return carry
-
-    lax.fori_loop(0, tiles, second_update, 0)
     gathered(7)
-
-    def last_update(i, carry):
+    for i in range(tiles):
         at = tile_at(i)
         out[at] = update(7, i, residual[at])
-        return carry
-
-    lax.fori_loop(0, tiles, last_update, 0)
 
     for u in range(4 * blocks):
         sent(u, 0, landing.at[u])
@@ -348,7 +323,7 @@
     anywhere = pl.BlockSpec(memory_space=pl.ANY)
     return pl.pallas_call(
         kernel,
-        out_shape=jax.ShapeDtypeStruct(targets.shape, f32),
+        out_shape=pltpu.VMEM(targets.shape, f32),
         in_specs=[pl.BlockSpec(memory_space=pltpu.SMEM)] + [anywhere] * 4,
         out_specs=pl.BlockSpec(memory_space=pltpu.VMEM),
         scratch_shapes=[
@@ -366,7 +341,8 @@
             pltpu.VMEM((blocks, rows, block), bf16),
             pltpu.VMEM((blocks, block, block), bf16),
             pltpu.VMEM((blocks, block, block), bf16),
-            pltpu.VMEM((block, block), f32),
+            pltpu.VMEM((block, rows), bf16),
+            pltpu.VMEM((block, rows), bf16),
             pltpu.VMEM((block, block), bf16),
             pltpu.VMEM((block, block), bf16),
             pltpu.VMEM((units, unit, lanes), f32),

time: 76.4 us -> 65.3 us (0.85)
  Pallas kernels: 73.3 us -> 63.5 us
  local copies, waits for them, and re-layouts: 2.26 us -> 0.97 us
    pallas_call x1, Pallas kernels: 73.3 us -> 63.5 us  [on_device(): pl.pallas_call(kernel, out_shape=pltpu.VMEM(targets.shape, f32), in_specs...]
    unnamed x1, local copies, waits for them, and re-layouts: 2.26 us -> 0.97 us
where the time goes in v3:
time: 65.3 us; the launch traced here: 65.2 us
  Pallas kernels  63.5 us (97%)
  local copies, waits for them, and re-layouts  0.97 us (1%)
  between operations  0.66 us (1%)
    pallas_call x1, Pallas kernels, on_device(): pl.pallas_call(kernel, out_shape=pltpu.VMEM(targets.shape, f32), in_specs...  63.5 us

profile of v3, /device:TPU:32, one launch (start us, length us, event | category | flops | bytes accessed | tf_op | source)
XLA Modules:
  0.0 65.2 jit_solution(8465756733727448656)
XLA Ops:
  0.7 63.5 %shard_map.55 = f32[2048,128]{1,0:T(8,128)S(1)} custom-call(s32[1]{0:T(128)S(6)} %copy.8.counts, s32[2,512]{1,0:T(2,128)} %ids_in.1, f32[2048,256]{1,0:T(8,128)} %samples_in.1, f32[2048,128]{1,0:T(8,128)} %targets_in.1, f32[2,512,512]{2,1,0:T(8,128)} %inverse_in.1), custom_call_target="tpu_custom_call" | custom-call | tf_op jit(solution)/shard_map/pallas_call | solution.py:324
  64.2 1.0 %copy.7 = f32[2048,128]{1,0:T(8,128)} copy(f32[2048,128]{1,0:T(8,128)S(1)} %shard_map.55) | data formatting | bytes 2097152

commit v4 on v3

--- a/solution.py
+++ b/solution.py
@@ -43,8 +43,8 @@
 
 
 def kernel(
-    counts, ids_in, samples_in, targets_in, inverse_in, out,
-    ids, samples, targets, inverse,
+    counts_in, ids_in, samples_in, targets_in, inverse_in, out,
+    counts, ids, samples, targets, inverse,
     x_high, x_low, r_turned, residual, p_high, p_low, c_high, c_low, b_high, b_low,
     turned_high, turned_low, cross_high, cross_low,
     part, landing, line, line_in, full, swapped,
@@ -71,13 +71,14 @@
     partner = (z, x, y, 1 - core)
 
     barrier = pltpu.get_barrier_semaphore()
+    for step in LINE_STEPS:
+        pl.semaphore_signal(barrier, inc=1, device_id=line_peer(step), device_id_type=MESH)
     for step in PLANE_STEPS:
         pl.semaphore_signal(barrier, inc=1, device_id=plane_peer(step)[0], device_id_type=MESH)
-    for step in LINE_STEPS:
-        pl.semaphore_signal(barrier, inc=1, device_id=line_peer(step), device_id_type=MESH)
     pl.semaphore_signal(barrier, inc=1, device_id=partner, device_id_type=MESH)
 
     chunk = rows // CHUNKS
+    counts_copy = pltpu.make_async_copy(counts_in, counts, in_sems.at[CHUNKS + 3])
     ids_copy = pltpu.make_async_copy(ids_in, ids, in_sems.at[CHUNKS])
     targets_copy = pltpu.make_async_copy(targets_in, targets, in_sems.at[CHUNKS + 1])
     inverse_copy = pltpu.make_async_copy(inverse_in, inverse, in_sems.at[CHUNKS + 2])
@@ -86,9 +87,12 @@
         at = pl.ds(n * chunk, chunk)
         return pltpu.make_async_copy(samples_in.at[at], samples.at[at], in_sems.at[n])
 
+    counts_copy.start()
     ids_copy.start()
     for n in range(CHUNKS):
         samples_copy(n).start()
+    targets_copy.start()
+    inverse_copy.start()
 
     def remote(src, dst, stage, device):
         return pltpu.make_async_remote_copy(
@@ -149,9 +153,8 @@
             return carry
 
         lax.fori_loop(n * per_chunk, (n + 1) * per_chunk, split_samples, 0)
-    targets_copy.start()
-    inverse_copy.start()
     ids_copy.wait()
+    counts_copy.wait()
 
     first = ((z * NX + x) * NY + y) * rows
 
@@ -163,13 +166,11 @@
         chosen = jnp.where(column == slots, 1.0, 0.0).astype(bf16)
         part[u] = dot(chosen, x_high[...], NN) + dot(chosen, x_low[...], NN)
 
-    pick(0)
+    for u in range(2 * blocks):
+        pick(u)
     pl.semaphore_wait(barrier, PLANE + NZ - 1)
     scatter(0)
-    pick(1)
     scatter(1)
-    pick(2)
-    pick(3)
 
     targets_copy.wait()
 
@@ -181,10 +182,6 @@
         return carry
 
     lax.fori_loop(0, tiles, turn_targets, 0)
-    to_line(0)
-    to_line(1)
-    scatter(2)
-    scatter(3)
 
     inverse_copy.wait()
     for b in range(blocks):
@@ -196,6 +193,10 @@
                 b_high[b, pl.ds(i * mine, mine), pl.ds(j * mine, mine)] = high
                 b_low[b, pl.ds(i * mine, mine), pl.ds(j * mine, mine)] = low
 
+    to_line(0)
+    to_line(1)
+    scatter(2)
+    scatter(3)
     gather(0, off_line(0))
     gather(1, off_line(1))
     to_line(2)
@@ -324,9 +325,10 @@
     return pl.pallas_call(
         kernel,
         out_shape=pltpu.VMEM(targets.shape, f32),
-        in_specs=[pl.BlockSpec(memory_space=pltpu.SMEM)] + [anywhere] * 4,
+        in_specs=[anywhere] * 5,
         out_specs=pl.BlockSpec(memory_space=pltpu.VMEM),
         scratch_shapes=[
+            pltpu.SMEM(counts.shape, jnp.int32),
             pltpu.VMEM(point_ids.shape, jnp.int32),
             pltpu.VMEM((rows, feat), f32),
             pltpu.VMEM((rows, wide), f32),
@@ -351,7 +353,7 @@
             pltpu.VMEM((units, NZ - 1, piece, lanes), f32),
             pltpu.VMEM((units, unit, lanes), f32),
             pltpu.VMEM((2 * blocks, unit, lanes), f32),
-            pltpu.SemaphoreType.DMA((CHUNKS + 3,)),
+            pltpu.SemaphoreType.DMA((CHUNKS + 4,)),
             pltpu.SemaphoreType.DMA((4 * units,)),
             pltpu.SemaphoreType.DMA((4 * units,)),
         ],

time: 65.3 us -> 65.4 us (level)
  no operation moved by 1% of the time
where the time goes in v4:
time: 65.4 us
  Pallas kernels  63.7 us (97%)
  local copies, waits for them, and re-layouts  0.97 us (1%)
  between operations  0.66 us (1%)
    pallas_call x1, Pallas kernels, on_device(): pl.pallas_call(kernel, out_shape=pltpu.VMEM(targets.shape, f32), in_specs...  63.7 us

profile of v4, /device:TPU:32, one launch (start us, length us, event | category | flops | bytes accessed | tf_op | source)
XLA Modules:
  0.0 65.4 jit_solution(14633469975710633465)
XLA Ops:
  0.7 63.7 %shard_map.55 = f32[2048,128]{1,0:T(8,128)S(1)} custom-call(s32[1]{0:T(128)S(6)} %copy.8.counts_in, s32[2,512]{1,0:T(2,128)} %ids_in.1, f32[2048,256]{1,0:T(8,128)} %samples_in.1, f32[2048,128]{1,0:T(8,128)} %targets_in.1, f32[2,512,512]{2,1,0:T(8,128)} %inverse_in.1), custom_call_target="tpu_custom_call" | custom-call | tf_op jit(solution)/shard_map/pallas_call | solution.py:325
  64.4 1.0 %copy.7 = f32[2048,128]{1,0:T(8,128)} copy(f32[2048,128]{1,0:T(8,128)S(1)} %shard_map.55) | data formatting | bytes 2097152

commit v5 on v4

--- a/solution.py
+++ b/solution.py
@@ -158,19 +158,20 @@
 
     first = ((z * NX + x) * NY + y) * rows
 
-    def pick(u):
-        start = pl.multiple_of(core * mine + (u % 2) * unit, unit)
-        wanted = ids[pl.ds(u // 2, 1), pl.ds(start, unit)] - first
-        column = jnp.broadcast_to(wanted.astype(f32), (8, unit)).T[:, :1]
-        slots = lax.broadcasted_iota(jnp.int32, (unit, rows), 1).astype(f32)
+    def pick(b):
+        wanted = ids[pl.ds(b, 1), pl.ds(pl.multiple_of(core * mine, mine), mine)] - first
+        column = jnp.broadcast_to(wanted.astype(f32), (8, mine)).T[:, :1]
+        slots = lax.broadcasted_iota(jnp.int32, (mine, rows), 1).astype(f32)
         chosen = jnp.where(column == slots, 1.0, 0.0).astype(bf16)
-        part[u] = dot(chosen, x_high[...], NN) + dot(chosen, x_low[...], NN)
-
-    for u in range(2 * blocks):
-        pick(u)
+        value = dot(chosen, x_high[...], NN) + dot(chosen, x_low[...], NN)
+        for n in range(2):
+            part[2 * b + n] = value[n * unit:(n + 1) * unit]
+
+    pick(0)
     pl.semaphore_wait(barrier, PLANE + NZ - 1)
     scatter(0)
     scatter(1)
+    pick(1)
 
     targets_copy.wait()
 
@@ -261,26 +262,33 @@
         sums(0, h)
         scatter(4 + h)
 
-    swap(2)
-    swap(3)
-    for h in range(2):
+    def second_columns(h):
         points_ready(1, h)
         for i in range(tiles):
             high, low = halves(columns(1, h, i).T)
             turned_high[pl.ds(h * mine, mine), tile_at(i)] = high
             turned_low[pl.ds(h * mine, mine), tile_at(i)] = low
-    to_line(4)
-    to_line(5)
-    for h in range(2):
+
+    def cross(h):
         at = pl.ds(h * mine, mine)
-        sums(1, h)
         value = (
             dot(turned_high[at], c_high[0], NN)
             + dot(turned_high[at], c_low[0], NN)
             + dot(turned_low[at], c_high[0], NN)
         )
         cross_high[at], cross_low[at] = halves(value)
+
+    swap(2)
+    swap(3)
+    second_columns(0)
+    to_line(4)
+    to_line(5)
+    second_columns(1)
+    sums(1, 0)
+    sums(1, 1)
+    cross(0)
     coefs(0)
+    cross(1)
 
     gathered(4)
     gathered(5)

time: 65.4 us -> 66.4 us (1.015)
  Pallas kernels: 63.7 us -> 64.7 us
    pallas_call x1, Pallas kernels: 63.7 us -> 64.7 us  [on_device(): pl.pallas_call(kernel, out_shape=pltpu.VMEM(targets.shape, f32), in_specs...]
where the time goes in v5:
time: 66.4 us; the launch traced here: 66.3 us
  Pallas kernels  64.7 us (97%)
  local copies, waits for them, and re-layouts  0.97 us (1%)
    pallas_call x1, Pallas kernels, on_device(): pl.pallas_call(kernel, out_shape=pltpu.VMEM(targets.shape, f32), in_specs...  64.7 us

profile of v5, /device:TPU:32, one launch (start us, length us, event | category | flops | bytes accessed | tf_op | source)
XLA Modules:
  0.0 66.3 jit_solution(6413645828981741685)
XLA Ops:
  0.7 64.7 %shard_map.55 = f32[2048,128]{1,0:T(8,128)S(1)} custom-call(s32[1]{0:T(128)S(6)} %copy.8.counts_in, s32[2,512]{1,0:T(2,128)} %ids_in.1, f32[2048,256]{1,0:T(8,128)} %samples_in.1, f32[2048,128]{1,0:T(8,128)} %targets_in.1, f32[2,512,512]{2,1,0:T(8,128)} %inverse_in.1), custom_call_target="tpu_custom_call" | custom-call | tf_op jit(solution)/shard_map/pallas_call | solution.py:333
  65.3 1.0 %copy.7 = f32[2048,128]{1,0:T(8,128)} copy(f32[2048,128]{1,0:T(8,128)S(1)} %shard_map.55) | data formatting | bytes 2097152

commit v6 on v5

--- a/solution.py
+++ b/solution.py
@@ -46,7 +46,7 @@
     counts_in, ids_in, samples_in, targets_in, inverse_in, out,
     counts, ids, samples, targets, inverse,
     x_high, x_low, r_turned, residual, p_high, p_low, c_high, c_low, b_high, b_low,
-    turned_high, turned_low, cross_high, cross_low,
+    turned_high, turned_low, cross_high, cross_low, solved_high, solved_low,
     part, landing, line, line_in, full, swapped,
     in_sems, send_sems, recv_sems,
 ):
@@ -238,15 +238,14 @@
         both = dot(c_high[b, tile_at(i), points], jnp.concatenate([high, low], axis=0), NT)
         return current - (both[:, :wide] + both[:, wide:] + dot(c_low[b, tile_at(i), points], high, NT))
 
-    def coefs(b):
-        first_unit = 2 * (blocks + b)
-        sums = jnp.concatenate([off_line(first_unit), off_line(first_unit + 1)], axis=1)
+    def coefs():
+        sums = jnp.concatenate([off_line(4), off_line(5)], axis=1)
         high, low = halves(sums)
         both = jnp.concatenate([high, low], axis=0)
         for h in range(2):
             at = pl.ds(h * mine, mine)
-            value = dot(both, b_high[b, at], NT)
-            gather(first_unit + h, value[:piece] + value[piece:] + dot(high, b_low[b, at], NT))
+            value = dot(both, b_high[0, at], NT)
+            gather(4 + h, value[:piece] + value[piece:] + dot(high, b_low[0, at], NT))
 
     swap(0)
     swap(1)
@@ -281,14 +280,26 @@
     swap(2)
     swap(3)
     second_columns(0)
+    second_columns(1)
     to_line(4)
     to_line(5)
-    second_columns(1)
     sums(1, 0)
     sums(1, 1)
     cross(0)
-    coefs(0)
     cross(1)
+    coefs()
+
+    early_high, early_low = halves(jnp.concatenate([part[6], part[7]], axis=1))
+    for h in range(2):
+        at = pl.ds(h * mine, mine)
+        solved_high[at], solved_low[at] = halves(
+            dot(b_high[1, at], cross_high[...], NN)
+            + dot(b_high[1, at], cross_low[...], NN)
+            + dot(b_low[1, at], cross_high[...], NN)
+        )
+        part[6 + h] = (
+            dot(early_high, b_high[1, at], NT) + dot(early_high, b_low[1, at], NT) + dot(early_low, b_high[1, at], NT)
+        )
 
     gathered(4)
     gathered(5)
@@ -296,8 +307,8 @@
     both = jnp.concatenate([high, low], axis=0)
     for h in range(2):
         at = pl.ds(h * mine, mine)
-        value = dot(both, cross_high[at], NT)
-        part[6 + h] -= value[:wide] + value[wide:] + dot(high, cross_low[at], NT)
+        value = dot(both, solved_high[at], NT)
+        part[6 + h] -= value[:wide] + value[wide:] + dot(high, solved_low[at], NT)
         scatter(6 + h)
 
     for i in range(tiles):
@@ -305,7 +316,8 @@
         residual[at] = update(5, i, update(4, i, targets[at]))
     to_line(6)
     to_line(7)
-    coefs(1)
+    gather(6, off_line(6))
+    gather(7, off_line(7))
     gathered(6)
     for i in range(tiles):
         at = tile_at(i)
@@ -355,6 +367,8 @@
             pltpu.VMEM((block, rows), bf16),
             pltpu.VMEM((block, block), bf16),
             pltpu.VMEM((block, block), bf16),
+            pltpu.VMEM((block, block), bf16),
+            pltpu.VMEM((block, block), bf16),
             pltpu.VMEM((units, unit, lanes), f32),
             pltpu.VMEM((units, PLANE - 1, piece, lanes), f32),
             pltpu.VMEM((units, piece, lanes), f32),

time: 66.4 us -> 64.2 us (0.967)
  Pallas kernels: 64.7 us -> 62.4 us
    pallas_call x1, Pallas kernels: 64.7 us -> 62.4 us  [on_device(): pl.pallas_call(kernel, out_shape=pltpu.VMEM(targets.shape, f32), in_specs...]
where the time goes in v6:
time: 64.2 us; the launch traced here: 64.1 us
  Pallas kernels  62.4 us (97%)
  local copies, waits for them, and re-layouts  0.97 us (2%)
  between operations  0.66 us (1%)
    pallas_call x1, Pallas kernels, on_device(): pl.pallas_call(kernel, out_shape=pltpu.VMEM(targets.shape, f32), in_specs...  62.4 us

profile of v6, /device:TPU:32, one launch (start us, length us, event | category | flops | bytes accessed | tf_op | source)
XLA Modules:
  0.0 64.1 jit_solution(6578869768774807911)
XLA Ops:
  0.7 62.4 %shard_map.55 = f32[2048,128]{1,0:T(8,128)S(1)} custom-call(s32[1]{0:T(128)S(6)} %copy.8.counts_in, s32[2,512]{1,0:T(2,128)} %ids_in.1, f32[2048,256]{1,0:T(8,128)} %samples_in.1, f32[2048,128]{1,0:T(8,128)} %targets_in.1, f32[2,512,512]{2,1,0:T(8,128)} %inverse_in.1), custom_call_target="tpu_custom_call" | custom-call | tf_op jit(solution)/shard_map/pallas_call | solution.py:345
  63.1 1.0 %copy.7 = f32[2048,128]{1,0:T(8,128)} copy(f32[2048,128]{1,0:T(8,128)S(1)} %shard_map.55) | data formatting | bytes 2097152

commit v7 on v6

--- a/solution.py
+++ b/solution.py
@@ -283,11 +283,11 @@
     second_columns(1)
     to_line(4)
     to_line(5)
-    sums(1, 0)
-    sums(1, 1)
     cross(0)
     cross(1)
     coefs()
+    sums(1, 0)
+    sums(1, 1)
 
     early_high, early_low = halves(jnp.concatenate([part[6], part[7]], axis=1))
     for h in range(2):

time: 64.2 us -> 67.5 us (1.051)
  Pallas kernels: 62.4 us -> 65.7 us
    pallas_call x1, Pallas kernels: 62.4 us -> 65.7 us  [on_device(): pl.pallas_call(kernel, out_shape=pltpu.VMEM(targets.shape, f32), in_specs...]
where the time goes in v7:
time: 67.5 us; the launch traced here: 67.3 us
  Pallas kernels  65.7 us (97%)
  local copies, waits for them, and re-layouts  0.97 us (1%)
    pallas_call x1, Pallas kernels, on_device(): pl.pallas_call(kernel, out_shape=pltpu.VMEM(targets.shape, f32), in_specs...  65.7 us

profile of v7, /device:TPU:32, one launch (start us, length us, event | category | flops | bytes accessed | tf_op | source)
XLA Modules:
  0.0 67.3 jit_solution(14891700248455568781)
XLA Ops:
  0.7 65.7 %shard_map.55 = f32[2048,128]{1,0:T(8,128)S(1)} custom-call(s32[1]{0:T(128)S(6)} %copy.8.counts_in, s32[2,512]{1,0:T(2,128)} %ids_in.1, f32[2048,256]{1,0:T(8,128)} %samples_in.1, f32[2048,128]{1,0:T(8,128)} %targets_in.1, f32[2,512,512]{2,1,0:T(8,128)} %inverse_in.1), custom_call_target="tpu_custom_call" | custom-call | tf_op jit(solution)/shard_map/pallas_call | solution.py:345
  66.4 1.0 %copy.7 = f32[2048,128]{1,0:T(8,128)} copy(f32[2048,128]{1,0:T(8,128)S(1)} %shard_map.55) | data formatting | bytes 2097152
